TPU v7x, 32 devices: a whole 2x2x4 slice. The times are simulated.
32 devices in a mesh: grp: 16 (over z, x, core), fsdp: 2 (over y).
Axes of the slice: x: 2, y: 2, z: 4, core: 2. Of those that a mesh axis runs over, the one named last changes fastest.
Arguments:
- tokens: bfloat16 [12288, 3584], P(('grp', 'fsdp')), may hold values from -6 to 6
- target: bfloat16 [12288, 1024], P(('grp', 'fsdp')), may hold values from -6 to 6
- weight: bfloat16 [3584, 1024], P('fsdp'), may hold values from -0.09375 to 0.09375
- factor_a: bfloat16 [3584, 512], P('fsdp'), may hold values from -6 to 6
- factor_b: bfloat16 [512, 1024], replicated, may hold values from -6 to 6
- counts: int32 [256], replicated, may hold values from 1 to 192, 12288 in all
- cand_index: int32 [256, 2], replicated, may hold values from 0 to 511
Outputs:
- update: float32 [3584, 1024], P('fsdp')
- scores: float32 [256], replicated
Inputs may be any that keep to these rules, and one draw needn't show every extreme that they name: The counts sum to 12288; candidate i owns the tokens from counts[0] + ... + counts[i-1] on.
All inputs are finite; a program needn't handle non-finite values.
Results may differ from a plain program's by a relative error of at most 0.003.
Values may be sent and summed in bfloat16 or wider, within the bound.
No kernel may reach another device: no remote copies, remote signals or barrier semaphores. Data moves between devices by JAX's collectives and lax.ppermute only.
A program may use at most 64 MiB of HBM per device.

v0:
```python
import jax
import jax.numpy as jnp
from jax import lax
from jax.sharding import PartitionSpec as P

D = 3584


def per_device(tokens, target, weight, factor_a, factor_b, counts, cand_index):
    rows = tokens.shape[0]
    width_out = weight.shape[1]
    pool_size = factor_a.shape[1]
    total_cands = counts.shape[0]
    noise = 0.5 * D ** (-0.5)
    spread_rows = lax.all_to_all(tokens, "fsdp", split_axis=1, concat_axis=0, tiled=True)
    joined = jnp.concatenate((weight, factor_a), axis=1)
    summed = lax.psum_scatter(
        jnp.dot(spread_rows, joined, preferred_element_type=jnp.float32),
        "fsdp",
        scatter_dimension=0,
        tiled=True,
    )
    base = summed[:, :width_out]
    pool_scores = summed[:, width_out:]
    ends = jnp.cumsum(counts)
    position = lax.axis_index(("grp", "fsdp")) * rows + jnp.arange(rows, dtype=jnp.int32)
    owner = jnp.sum((ends[None, :] <= position[:, None]).astype(jnp.int32), axis=1)
    left_index = cand_index[:, 0]
    right_index = cand_index[:, 1]
    tok_a = jnp.take(left_index, owner)
    tok_b = jnp.take(right_index, owner)
    pool_ids = jnp.arange(pool_size, dtype=jnp.int32)
    picked = jnp.sum(jnp.where(tok_a[:, None] == pool_ids[None, :], pool_scores, 0.0), axis=1)
    right_rows = jnp.take(factor_b, tok_b, axis=0).astype(jnp.float32)
    output = base + noise * picked[:, None] * right_rows
    diff = output - target.astype(jnp.float32)
    loss = jnp.mean(diff * diff, axis=1)
    cand_ids = jnp.arange(total_cands, dtype=jnp.int32)
    partial_value = jnp.sum(
        jnp.where(owner[:, None] == cand_ids[None, :], loss[:, None], 0.0), axis=0
    )
    totals = lax.psum(partial_value, ("grp", "fsdp"))
    fitness = -totals / counts.astype(jnp.float32)
    middle = jnp.mean(fitness)
    variance = jnp.mean((fitness - middle) ** 2)
    scores = (fitness - middle) / jnp.sqrt(variance + 1e-06)
    selector = (pool_ids[:, None] == left_index[None, :]).astype(jnp.bfloat16)
    columns = jnp.dot(factor_a, selector, preferred_element_type=jnp.float32)
    scaled = (columns * scores[None, :]).astype(jnp.bfloat16)
    chosen_rows = jnp.take(factor_b, right_index, axis=0)
    summed_update = jnp.dot(scaled, chosen_rows, preferred_element_type=jnp.float32)
    update = summed_update / jnp.sqrt(jnp.float32(total_cands))
    return (update, scores)


def solution(mesh):
    in_specs = (
        P(("grp", "fsdp"), None),
        P(("grp", "fsdp"), None),
        P("fsdp", None),
        P("fsdp", None),
        P(),
        P(),
        P(),
    )
    out_specs = (P("fsdp", None), P())
    return jax.shard_map(
        per_device, mesh=mesh, in_specs=in_specs, out_specs=out_specs, check_vma=False
    )
```

profile of v0, /device:TPU:0, one launch (start us, length us, event | category | flops | bytes accessed | tf_op | source)
XLA Modules:
  0.0 185.1 jit_solution(5749809767784370416)
XLA Ops:
  7.2 0.0 copy-start
  7.2 0.0 reduce-scatter.2.cloned.1.call-start
  7.2 4.6 %copy.17 = bf16[384,3584]{0,1:T(8,128)(2,1)} copy(bf16[384,3584]{1,0:T(8,128)(2,1)} %param.9) | data formatting | bytes 5505024 | tf_op args[0]
  11.8 39.5 %all_to_all.19 = bf16[384,2,1792]{0,2,1:T(8,128)(2,1)} all-to-all(bf16[384,2,1792]{0,2,1:T(8,128)(2,1)} %bitcast.17), channel_id=1, replica_groups=mesh['grp'=16,'fsdp'=2] {'fsdp'}, dimensions={1} | all-to-all | bytes 5505024 | tf_op jit(solution)/shard_map/all_to_all | solution.py:15
  51.3 4.8 %copy.18 = bf16[2,384,1792]{2,1,0:T(8,128)(2,1)} copy(bf16[2,384,1792]{1,2,0:T(8,128)(2,1)} %bitcast.16) | data formatting | bytes 5505024 | tf_op jit(solution)/shard_map/all_to_all | solution.py:15
  56.1 0.0 copy-done.1
  56.1 9.6 %fusion.4 = f32[768,1536]{0,1:T(8,128)} fusion(bf16[768,1792]{1,0:T(8,128)(2,1)} %bitcast.18, bf16[1792,512]{1,0:T(8,128)(2,1)S(1)} %copy-done.1, bf16[1792,1024]{1,0:T(8,128)(2,1)} %param.11), kind=kOutput, calls=%fused_computation.9 | convolution fusion | flops 4238868480 | bytes 12976128 | tf_op jit(solution)/shard_map/dot_general | solution.py:18
  65.7 0.0 reduce-scatter.2.cloned.1.call-update
  65.7 0.6 copy-done.4
  66.4 0.3 reduce-window.9
  66.7 0.1 slice.20
  66.8 0.1 slice_reduce_fusion
  66.9 0.1 add_bitcast_fusion
  67.0 0.2 convert_reduce_fusion
  67.3 0.0 copy-done.3
  67.3 2.8 %gather_fusion.2 = s32[384]{0:T(512)S(1)} fusion(s32[256]{0:T(256)S(1)} %bitcast.13, s32[1024]{0:T(1024)S(1)} %pad_clamp_fusion.2), kind=kCustom, calls=%fused_computation.clone | custom fusion | bytes 4608 | tf_op jit(solution)/shard_map/jit(_take)/gather | solution.py:30
  70.1 2.8 %gather_fusion.3 = s32[384]{0:T(512)S(1)} fusion(s32[256]{0:T(256)S(1)} %bitcast.15, s32[1024]{0:T(1024)S(1)} %pad_clamp_fusion.2), kind=kCustom, calls=%fused_computation.1.clone | custom fusion | bytes 4608 | tf_op jit(solution)/shard_map/jit(_take)/gather | solution.py:31
  72.9 0.0 copy-start.2
  73.0 2.1 %gather_fusion = bf16[384,1024]{1,0:T(8,128)(2,1)S(1)} fusion(bf16[512,1024]{1,0:T(8,128)(2,1)S(1)} %copy-done, s32[1024]{0:T(1024)S(1)} %pad_clamp_fusion.1), kind=kCustom, calls=%fused_computation.2 | custom fusion | bytes 1574400 | tf_op jit(solution)/shard_map/jit(_take)/gather | solution.py:34
  75.0 0.4 copy.19
  75.4 0.0 copy-done.2
  75.4 0.4 copy.20
  75.8 1.2 gather_fusion.1
  77.0 49.5 %reduce-scatter.2.cloned.1.call-done = f32[384,1536]{0,1:T(8,128)} async-done(((f32[768,1536]{0,1:T(8,128)}), f32[384,1536]{0,1:T(8,128)}) %reduce-scatter.2.cloned.1.call-update) | async-done | bytes 2359312 | tf_op jit(solution)/shard_map/reduce_scatter | solution.py:17
  126.5 1.3 fusion.12
  127.7 1.9 fusion.10
  129.6 0.2 select_reduce_fusion
  129.8 39.5 %psum.7 = f32[256]{0:T(256)S(1)} all-reduce(f32[256]{0:T(256)S(1)} %select_reduce_fusion), channel_id=1, replica_groups=mesh['grp'=16,'fsdp'=2] {'grp','fsdp'}, use_global_device_ids=true, to_apply=%region_7.9 | all-reduce | flops 256 | bytes 2048 | tf_op jit(solution)/shard_map/psum | solution.py:42
  169.3 0.6 fusion.23
  170.5 0.6 multiply_reduce_fusion
  171.8 0.0 copy-start.5
  171.9 6.4 %convolution_multiply_fusion = f32[1792,1024]{1,0:T(8,128)} fusion(bf16[1792,512]{1,0:T(8,128)(2,1)} %param.12, f32[256]{0:T(256)S(1)} %subtract_divide_fusion, bf16[256,1024]{1,0:T(8,128)(2,1)S(1)} %gather_fusion.1, pred[256]{0:T(512)(128)(4,1)S(1)} %get-tuple-element.3, s32[256]{0:T(256)S(1)} %bitcast.14), kind=kOutput, calls=%fused_computation.8 | convolution fusion | flops 1412562944 | bytes 9701632 | tf_op jit(solution)/shard_map/dot_general | solution.py:51
  (18 shorter events, 0.1 us)
Async XLA Ops:
  7.2 65.8 %copy-start = (bf16[512,1024]{1,0:T(8,128)(2,1)S(1)}, bf16[512,1024]{1,0:T(8,128)(2,1)}, u32[]{:S(2)}) copy-start(bf16[512,1024]{1,0:T(8,128)(2,1)} %param.13) | copy-start | bytes 3145732
  7.2 119.3 %reduce-scatter.2.cloned.1.call-start = ((), (), s32[]{:S(2)}) async-start(), calls=%async_computation.2 | async-start | bytes 7077888 | tf_op jit(solution)/shard_map/reduce_scatter | solution.py:17
  51.3 4.8 %copy-start.1 = (bf16[1792,512]{1,0:T(8,128)(2,1)S(1)}, bf16[1792,512]{1,0:T(8,128)(2,1)}, u32[]{:S(2)}) copy-start(bf16[1792,512]{1,0:T(8,128)(2,1)} %param.12) | copy-start | bytes 5505028
  65.7 0.7 copy-start.4
  65.7 1.5 copy-start.3
  72.9 2.5 %copy-start.2 = (bf16[384,1024]{1,0:T(8,128)(2,1)S(1)}, bf16[384,1024]{1,0:T(8,128)(2,1)}, u32[]{:S(2)}) copy-start(bf16[384,1024]{1,0:T(8,128)(2,1)} %param.10) | copy-start | bytes 2359300
  171.8 6.4 %copy-start.5 = (f32[256]{0:T(256)}, f32[256]{0:T(256)S(1)}, u32[]{:S(2)}) copy-start(f32[256]{0:T(256)S(1)} %subtract_divide_fusion) | copy-start | bytes 3076
Sparse Core Ops, SparseCore 0:
  65.9 60.5 reduce-scatter.1
where the time goes:
time: 186 us; the launch traced here: 185 us
  blocking collectives  79 us (42%)
  waiting for transfers between devices  49.5 us (27%)
  local copies, waits for them, and re-layouts  19.8 us (11%)
  matrix products  16 us (9%)
  between operations  15.5 us (8%)
  other arithmetic  5.24 us (3%)
    reduce_scatter x1, waiting for transfers between devices, per_device(): lax.psum_scatter(jnp.dot(spread_rows, joined, preferred_element_type=jnp....  49.5 us
    all_to_all x1, blocking collectives, per_device(): lax.all_to_all(tokens, 'fsdp', split_axis=1, concat_axis=0, tiled=True)  39.5 us
    psum x1, blocking collectives, per_device(): totals = lax.psum(partial_value, ('grp', 'fsdp'))  39.5 us
    dot_general x1, matrix products, per_device(): jnp.dot(spread_rows, joined, preferred_element_type=jnp.float32)  9.63 us
    dot_general x1, matrix products, per_device(): jnp.dot(scaled, chosen_rows, preferred_element_type=jnp.float32)  6.42 us
    unnamed x14, local copies, waits for them, and re-layouts  5.6 us
    all_to_all x1, local copies, waits for them, and re-layouts, per_device(): lax.all_to_all(tokens, 'fsdp', split_axis=1, concat_axis=0, tiled=True)  4.77 us
  transfers between devices with their start and end apart: 1, of which 1 were waited for; matrix products, arithmetic and copies ran while one was open for 6% of the time, Pallas kernels for 0%

commit v1 on v0

--- a/solution.py
+++ b/solution.py
@@ -39,7 +39,7 @@
     partial_value = jnp.sum(
         jnp.where(owner[:, None] == cand_ids[None, :], loss[:, None], 0.0), axis=0
     )
-    totals = lax.psum(partial_value, ("grp", "fsdp"))
+    totals = jnp.sum(lax.all_gather(partial_value, ("grp", "fsdp")), axis=0)
     fitness = -totals / counts.astype(jnp.float32)
     middle = jnp.mean(fitness)
     variance = jnp.mean((fitness - middle) ** 2)

time: 186 us -> 213 us (1.15)
  blocking collectives: 79 us -> 106 us
    all_gather x0 -> x1, blocking collectives: none -> 66.9 us  [per_device(): totals = jnp.sum(lax.all_gather(partial_value, ('grp', 'fsdp')), axis=0)]
    psum x1 -> x0, blocking collectives: 39.5 us -> none  [per_device(): totals = lax.psum(partial_value, ('grp', 'fsdp'))]
  transfers between devices with their start and end apart: 1 -> 1, of which waited for: 1 -> 1; matrix products, arithmetic and copies ran while one was open for 6% -> 5% of each run, Pallas kernels for 0% -> 0%
where the time goes in v1:
time: 213 us
  blocking collectives  106 us (50%)
  waiting for transfers between devices  49.5 us (23%)
  local copies, waits for them, and re-layouts  19.8 us (9%)
  matrix products  16.1 us (8%)
  between operations  15.5 us (7%)
  other arithmetic  5.3 us (2%)
    all_gather x1, blocking collectives, per_device(): totals = jnp.sum(lax.all_gather(partial_value, ('grp', 'fsdp')), axis=0)  66.9 us
    reduce_scatter x1, waiting for transfers between devices, per_device(): lax.psum_scatter(jnp.dot(spread_rows, joined, preferred_element_type=jnp....  49.5 us
    all_to_all x1, blocking collectives, per_device(): lax.all_to_all(tokens, 'fsdp', split_axis=1, concat_axis=0, tiled=True)  39.5 us
    dot_general x1, matrix products, per_device(): jnp.dot(spread_rows, joined, preferred_element_type=jnp.float32)  9.63 us
    dot_general x1, matrix products, per_device(): jnp.dot(scaled, chosen_rows, preferred_element_type=jnp.float32)  6.43 us
    unnamed x14, local copies, waits for them, and re-layouts  5.6 us
    all_to_all x1, local copies, waits for them, and re-layouts, per_device(): lax.all_to_all(tokens, 'fsdp', split_axis=1, concat_axis=0, tiled=True)  4.77 us
  transfers between devices with their start and end apart: 1, of which 1 were waited for; matrix products, arithmetic and copies ran while one was open for 5% of the time, Pallas kernels for 0%

profile of v1, /device:TPU:0, one launch (start us, length us, event | category | flops | bytes accessed | tf_op | source)
XLA Modules:
  0.0 212.6 jit_solution(4402080190296923553)
XLA Ops:
  7.2 0.0 copy-start
  7.2 0.0 reduce-scatter.2.cloned.1.call-start
  7.2 4.6 %copy.21 = bf16[384,3584]{0,1:T(8,128)(2,1)} copy(bf16[384,3584]{1,0:T(8,128)(2,1)} %param.9) | data formatting | bytes 5505024 | tf_op args[0]
  11.8 39.5 %all_to_all.19 = bf16[384,2,1792]{0,2,1:T(8,128)(2,1)} all-to-all(bf16[384,2,1792]{0,2,1:T(8,128)(2,1)} %bitcast.18), channel_id=1, replica_groups=mesh['grp'=16,'fsdp'=2] {'fsdp'}, dimensions={1} | all-to-all | bytes 5505024 | tf_op jit(solution)/shard_map/all_to_all | solution.py:15
  51.3 4.8 %copy.22 = bf16[2,384,1792]{2,1,0:T(8,128)(2,1)} copy(bf16[2,384,1792]{1,2,0:T(8,128)(2,1)} %bitcast.17) | data formatting | bytes 5505024 | tf_op jit(solution)/shard_map/all_to_all | solution.py:15
  56.1 0.0 copy-done.1
  56.1 9.6 %fusion.4 = f32[768,1536]{0,1:T(8,128)} fusion(bf16[768,1792]{1,0:T(8,128)(2,1)} %bitcast.19, bf16[1792,512]{1,0:T(8,128)(2,1)S(1)} %copy-done.1, bf16[1792,1024]{1,0:T(8,128)(2,1)} %param.11), kind=kOutput, calls=%fused_computation.9 | convolution fusion | flops 4238868480 | bytes 12976128 | tf_op jit(solution)/shard_map/dot_general | solution.py:18
  65.7 0.0 reduce-scatter.2.cloned.1.call-update
  65.8 0.6 copy-done.4
  66.4 0.3 reduce-window.9
  66.7 0.1 slice.20
  66.8 0.1 slice_reduce_fusion
  66.9 0.1 add_bitcast_fusion
  67.0 0.2 convert_reduce_fusion
  67.3 0.0 copy-done.3
  67.3 2.8 %gather_fusion.2 = s32[384]{0:T(512)S(1)} fusion(s32[256]{0:T(256)S(1)} %bitcast.14, s32[1024]{0:T(1024)S(1)} %pad_clamp_fusion.2), kind=kCustom, calls=%fused_computation.clone | custom fusion | bytes 4608 | tf_op jit(solution)/shard_map/jit(_take)/gather | solution.py:30
  70.1 2.8 %gather_fusion.3 = s32[384]{0:T(512)S(1)} fusion(s32[256]{0:T(256)S(1)} %bitcast.16, s32[1024]{0:T(1024)S(1)} %pad_clamp_fusion.2), kind=kCustom, calls=%fused_computation.1.clone | custom fusion | bytes 4608 | tf_op jit(solution)/shard_map/jit(_take)/gather | solution.py:31
  73.0 0.0 copy-start.2
  73.0 2.1 gather_fusion
  75.0 0.4 copy.23
  75.4 0.4 copy.24
  75.8 1.2 gather_fusion.1
  77.0 49.5 %reduce-scatter.2.cloned.1.call-done = f32[384,1536]{0,1:T(8,128)} async-done(((f32[768,1536]{0,1:T(8,128)}), f32[384,1536]{0,1:T(8,128)}) %reduce-scatter.2.cloned.1.call-update) | async-done | bytes 2359312 | tf_op jit(solution)/shard_map/reduce_scatter | solution.py:17
  126.5 1.3 fusion.12
  127.7 1.9 fusion.10
  129.6 0.2 select_reduce_fusion
  129.8 66.9 %all-gather.1 = f32[32,1,256]{2,1,0:T(1,128)S(1)} all-gather(f32[1,1,256]{2,1,0:T(1,128)S(1)} %bitcast.20), channel_id=2, replica_groups=mesh['grp'=16,'fsdp'=2] {'grp','fsdp'}, dimensions={0}, use_global_device_ids=true | all-gather | bytes 33792 | tf_op jit(solution)/shard_map/all_gather | solution.py:42
  196.7 0.1 reduce_sum.67
  196.8 0.6 fusion.23
  198.0 0.6 multiply_reduce_fusion
  199.3 0.0 copy-start.5
  199.4 6.4 %convolution_multiply_fusion = f32[1792,1024]{1,0:T(8,128)} fusion(bf16[1792,512]{1,0:T(8,128)(2,1)} %param.12, f32[256]{0:T(256)S(1)} %subtract_divide_fusion, bf16[256,1024]{1,0:T(8,128)(2,1)S(1)} %gather_fusion.1, pred[256]{0:T(512)(128)(4,1)S(1)} %get-tuple-element.3, s32[256]{0:T(256)S(1)} %bitcast.15), kind=kOutput, calls=%fused_computation.8 | convolution fusion | flops 1412562944 | bytes 9701632 | tf_op jit(solution)/shard_map/dot_general | solution.py:51
  (19 shorter events, 0.1 us)
Async XLA Ops:
  7.2 65.8 %copy-start = (bf16[512,1024]{1,0:T(8,128)(2,1)S(1)}, bf16[512,1024]{1,0:T(8,128)(2,1)}, u32[]{:S(2)}) copy-start(bf16[512,1024]{1,0:T(8,128)(2,1)} %param.13) | copy-start | bytes 3145732
  7.2 119.3 %reduce-scatter.2.cloned.1.call-start = ((), (), s32[]{:S(2)}) async-start(), calls=%async_computation.2 | async-start | bytes 7077888 | tf_op jit(solution)/shard_map/reduce_scatter | solution.py:17
  51.3 4.8 %copy-start.1 = (bf16[1792,512]{1,0:T(8,128)(2,1)S(1)}, bf16[1792,512]{1,0:T(8,128)(2,1)}, u32[]{:S(2)}) copy-start(bf16[1792,512]{1,0:T(8,128)(2,1)} %param.12) | copy-start | bytes 5505028
  65.7 0.7 copy-start.4
  65.7 1.5 copy-start.3
  73.0 2.5 %copy-start.2 = (bf16[384,1024]{1,0:T(8,128)(2,1)S(1)}, bf16[384,1024]{1,0:T(8,128)(2,1)}, u32[]{:S(2)}) copy-start(bf16[384,1024]{1,0:T(8,128)(2,1)} %param.10) | copy-start | bytes 2359300
  199.3 6.4 %copy-start.5 = (f32[256]{0:T(256)}, f32[256]{0:T(256)S(1)}, u32[]{:S(2)}) copy-start(f32[256]{0:T(256)S(1)} %subtract_divide_fusion) | copy-start | bytes 3076
Sparse Core Ops, SparseCore 0:
  65.9 60.5 reduce-scatter.1
